TPU v7x, 256 devices: a whole 4x4x8 slice. The times are simulated.
256 devices in a mesh: replica: 64 (over z, y, core), model: 4 (over x).
Axes of the slice: x: 4, y: 4, z: 8, core: 2. Of those that a mesh axis runs over, the one named last changes fastest.
Arguments:
- slope_query: bfloat16 [64, 1024, 1024], P('replica', None, 'model'), may hold values from -8 to 8
- slope_key: bfloat16 [64, 1024, 1024], P('replica', None, 'model'), may hold values from -8 to 8
- slope_value: bfloat16 [64, 1024, 1024], P('replica', None, 'model'), may hold values from -8 to 8
- slope_mixed: bfloat16 [64, 1024, 1024], P('replica', 'model'), may hold values from -8 to 8
- slope_norm: bfloat16 [64, 1024], P('replica'), may hold values from -16 to 16
- param_query: float32 [1024, 1024], P('replica', 'model'), may hold values from -0.5 to 0.5
- param_key: float32 [1024, 1024], P('replica', 'model'), may hold values from -0.5 to 0.5
- param_value: float32 [1024, 1024], P('replica', 'model'), may hold values from -0.5 to 0.5
- param_mixed: float32 [1024, 1024], P('model', 'replica'), may hold values from -0.5 to 0.5
- param_norm: float32 [1024], P('replica'), may hold values from 0.25 to 1.75
- state_query: float32 [1024, 1024], P('replica', 'model'), may hold values from 0.0001953125 to 0.001953125
- state_key: float32 [1024, 1024], P('replica', 'model'), may hold values from 0.0001953125 to 0.001953125
- state_value: float32 [1024, 1024], P('replica', 'model'), may hold values from 0.0001953125 to 0.001953125
- state_mixed: float32 [1024, 1024], P('model', 'replica'), may hold values from 0.0001953125 to 0.001953125
- state_norm: float32 [1024], P('replica'), may hold values from 0.05 to 0.8
Outputs:
- half_query: bfloat16 [1024, 1024], P(None, 'model')
- half_key: bfloat16 [1024, 1024], P(None, 'model')
- half_value: bfloat16 [1024, 1024], P(None, 'model')
- half_mixed: bfloat16 [1024, 1024], P('model')
- half_norm: bfloat16 [1024], replicated
- next_query: float32 [1024, 1024], P('replica', 'model')
- next_key: float32 [1024, 1024], P('replica', 'model')
- next_value: float32 [1024, 1024], P('replica', 'model')
- next_mixed: float32 [1024, 1024], P('model', 'replica')
- next_norm: float32 [1024], P('replica')
- state_new_query: float32 [1024, 1024], P('replica', 'model')
- state_new_key: float32 [1024, 1024], P('replica', 'model')
- state_new_value: float32 [1024, 1024], P('replica', 'model')
- state_new_mixed: float32 [1024, 1024], P('model', 'replica')
- state_new_norm: float32 [1024], P('replica')
All inputs are finite; a program needn't handle non-finite values.
Results may differ from a plain program's by a relative error of at most 0.001.
Values may be sent and summed in bfloat16 or wider, within the bound.
No kernel may reach another device: no remote copies, remote signals or barrier semaphores. Data moves between devices by JAX's collectives and lax.ppermute only.
A program may use at most 64 MiB of HBM per device.

v0:
```python
import jax
import jax.numpy as jnp
from jax import lax
from jax.sharding import PartitionSpec as P

learn_rate = 0.025
hold_rate = 0.7


def in_blocks(value, dim, count):
    before, after = (value.shape[:dim], value.shape[dim + 1 :])
    return jnp.moveaxis(value.reshape(*before, count, -1, *after), dim, 0)


def sum_together(arrays, axis, dims):
    count = lax.axis_size(axis)
    blocks = [in_blocks(a, dim, count) for a, dim in zip(arrays, dims)]
    lines = jnp.concatenate([b.reshape(count, -1) for b in blocks], axis=1)
    rows = max(16, -(-lines.shape[1] // 1024) * 8)
    lines = jnp.pad(lines, ((0, 0), (0, rows * 128 - lines.shape[1]))).reshape(-1, 128)
    vector, at, gathered = (lax.psum_scatter(lines, axis, tiled=True).reshape(-1), 0, [])
    for b in blocks:
        part = b[0]
        gathered.append(vector[at : at + part.size].reshape(part.shape))
        at += part.size
    return tuple(gathered)


def sent_to_all(value, axis):
    copies = jnp.broadcast_to(value, (lax.axis_size(axis), *value.shape))
    return lax.all_to_all(copies, axis, split_axis=0, concat_axis=0, tiled=True)


def of_everyone(value, axis):
    everything = sent_to_all(value, axis)
    return jnp.sum(everything, axis=0)


def packed_total(arrays, axis):
    ends = [0]
    for a in arrays:
        ends.append(ends[-1] + a.size)
    total = of_everyone(jnp.concatenate([a.ravel() for a in arrays]), axis)
    return tuple((total[b:e].reshape(a.shape) for a, b, e in zip(arrays, ends, ends[1:])))


def turned_gather(arrays, axis, dims):
    turned = [jnp.moveaxis(a, dim, 0) for a, dim in zip(arrays, dims)]
    widths = [t[0].size for t in turned]
    both = jnp.concatenate([t.reshape(-1, w) for t, w in zip(turned, widths)], axis=1)
    result = lax.all_gather(both, axis, axis=0, tiled=True)
    blocks = jnp.split(result, [sum(widths[:k]) for k in range(1, len(widths))], axis=1)
    return tuple(
        (
            jnp.moveaxis(b.reshape(-1, *t.shape[1:]), 0, dim)
            for b, t, dim in zip(blocks, turned, dims)
        )
    )


def local(
    slope_query,
    slope_key,
    slope_value,
    slope_mixed,
    slope_norm,
    param_query,
    param_key,
    param_value,
    param_mixed,
    param_norm,
    state_query,
    state_key,
    state_value,
    state_mixed,
    state_norm,
):
    mean_query, mean_key, mean_value, mean_mixed, mean_norm = sum_together(
        (
            slope_query[0].astype(jnp.float32),
            slope_key[0].astype(jnp.float32),
            slope_value[0].astype(jnp.float32),
            slope_mixed[0].astype(jnp.float32),
            slope_norm[0].astype(jnp.float32),
        ),
        "replica",
        (0, 0, 0, 1, 0),
    )
    mean_rate = lax.axis_size("replica") ** (-0.5)
    mean_query = mean_query * mean_rate
    mean_key = mean_key * mean_rate
    mean_value = mean_value * mean_rate
    mean_mixed = mean_mixed * mean_rate
    mean_norm = mean_norm * mean_rate
    (
        own_query,
        own_key,
        own_value,
        own_mixed,
        slope_query_norm,
        slope_key_norm,
        slope_value_norm,
        slope_mixed_norm,
    ) = packed_total(
        (
            jnp.sum(param_query * param_query, axis=1, keepdims=True),
            jnp.sum(param_key * param_key, axis=1, keepdims=True),
            jnp.sum(param_value * param_value, axis=1, keepdims=True),
            jnp.sum(param_mixed * param_mixed, axis=0, keepdims=True),
            jnp.sum(mean_query * mean_query, axis=1, keepdims=True),
            jnp.sum(mean_key * mean_key, axis=1, keepdims=True),
            jnp.sum(mean_value * mean_value, axis=1, keepdims=True),
            jnp.sum(mean_mixed * mean_mixed, axis=0, keepdims=True),
        ),
        "model",
    )
    mean_query = mean_query * (jnp.sqrt(own_query) * lax.rsqrt(slope_query_norm + 1e-06))
    mean_key = mean_key * (jnp.sqrt(own_key) * lax.rsqrt(slope_key_norm + 1e-06))
    mean_value = mean_value * (jnp.sqrt(own_value) * lax.rsqrt(slope_value_norm + 1e-06))
    mean_mixed = mean_mixed * (jnp.sqrt(own_mixed) * lax.rsqrt(slope_mixed_norm + 1e-06))
    state_new_query = hold_rate * state_query + (1.0 - hold_rate) * mean_query * mean_query
    next_query = param_query - learn_rate * mean_query * lax.rsqrt(state_new_query + 1e-06)
    state_new_key = hold_rate * state_key + (1.0 - hold_rate) * mean_key * mean_key
    next_key = param_key - learn_rate * mean_key * lax.rsqrt(state_new_key + 1e-06)
    state_new_value = hold_rate * state_value + (1.0 - hold_rate) * mean_value * mean_value
    next_value = param_value - learn_rate * mean_value * lax.rsqrt(state_new_value + 1e-06)
    state_new_mixed = hold_rate * state_mixed + (1.0 - hold_rate) * mean_mixed * mean_mixed
    next_mixed = param_mixed - learn_rate * mean_mixed * lax.rsqrt(state_new_mixed + 1e-06)
    state_new_norm = hold_rate * state_norm + (1.0 - hold_rate) * mean_norm * mean_norm
    next_norm = param_norm - learn_rate * mean_norm * lax.rsqrt(state_new_norm + 1e-06)
    half_query, half_key, half_value, half_mixed, half_norm = turned_gather(
        (
            next_query.astype(jnp.bfloat16),
            next_key.astype(jnp.bfloat16),
            next_value.astype(jnp.bfloat16),
            next_mixed.astype(jnp.bfloat16),
            next_norm.astype(jnp.bfloat16),
        ),
        "replica",
        (0, 0, 0, 1, 0),
    )
    return (
        half_query,
        half_key,
        half_value,
        half_mixed,
        half_norm,
        next_query,
        next_key,
        next_value,
        next_mixed,
        next_norm,
        state_new_query,
        state_new_key,
        state_new_value,
        state_new_mixed,
        state_new_norm,
    )


def solution(mesh):
    return jax.shard_map(
        local,
        mesh=mesh,
        in_specs=(
            P("replica", None, "model"),
            P("replica", None, "model"),
            P("replica", None, "model"),
            P("replica", "model", None),
            P("replica", None),
            P("replica", "model"),
            P("replica", "model"),
            P("replica", "model"),
            P("model", "replica"),
            P("replica"),
            P("replica", "model"),
            P("replica", "model"),
            P("replica", "model"),
            P("model", "replica"),
            P("replica"),
        ),
        out_specs=(
            P(None, "model"),
            P(None, "model"),
            P(None, "model"),
            P("model", None),
            P(),
            P("replica", "model"),
            P("replica", "model"),
            P("replica", "model"),
            P("model", "replica"),
            P("replica"),
            P("replica", "model"),
            P("replica", "model"),
            P("replica", "model"),
            P("model", "replica"),
            P("replica"),
        ),
        check_vma=False,
    )
```

profile of v0, /device:TPU:1, one launch (start us, length us, event | category | flops | bytes accessed | tf_op | source)
XLA Modules:
  0.0 329.9 jit_solution(10158640224522271844)
XLA Ops:
  7.2 1.3 convert_element_type.42
  8.6 1.0 convert_element_type.43
  9.7 2.1 convert_element_type.44
  11.8 1.0 copy.76
  12.8 2.6 copy.77
  15.4 1.1 copy.78
  16.6 1.1 constant_dynamic-update-slice_fusion.3
  17.8 1.1 constant_dynamic-update-slice_fusion.2
  18.9 2.4 pad_convert_fusion
  21.3 5.0 %reshape.132 = f32[8704,128]{1,0:T(8,128)} reshape(f32[64,17408]{1,0:T(8,128)} %pad_convert_fusion) | data formatting | bytes 8912896 | tf_op jit(solution)/shard_map/reshape | solution.py:20
  28.6 196.8 %all-reduce.4.cloned.1.call-done = f32[8704,128]{1,0:T(8,128)} async-done(((f32[8704,128]{1,0:T(8,128)}), f32[8704,128]{1,0:T(8,128)}) %all-reduce.4.cloned.1.call-update) | async-done | bytes 4456464
  225.4 1.0 multiply_reduce_fusion.1
  227.8 4.0 %all-to-all-start = ((f32[4,1,128]{2,1,0:T(1,128)}), f32[4,1,128]{2,1,0:T(1,128)S(1)}, u32[]{:S(2)}, u32[]{:S(2)}) async-start(f32[4,1,128]{2,1,0:T(1,128)} %broadcast_in_dim.3), calls=%async_computation | async-start | bytes 4096 | tf_op jit(solution)/shard_map/all_to_all | solution.py:31
  231.8 0.9 dynamic-slice_bitcast_fusion
  233.4 2.4 all-to-all-done
  236.0 0.7 constant_dynamic-update-slice_fusion.9
  236.7 0.7 constant_dynamic-update-slice_fusion.8
  237.4 0.7 constant_dynamic-update-slice_fusion.7
  238.1 0.7 constant_dynamic-update-slice_fusion.6
  238.8 0.6 copy-done.7
  239.4 78.3 %all-gather.2.cloned.1.call-done = bf16[1024,1025]{1,0:T(8,128)(2,1)} async-done(((bf16[16,1025]{1,0:T(8,128)(2,1)}), bf16[1024,1025]{1,0:T(8,128)(2,1)}) %all-gather.2.cloned.1.call-update) | async-done | bytes 2099216 | tf_op jit(solution)/shard_map/all_gather | solution.py:51
  317.7 2.7 slice_bitcast_fusion
  320.4 1.0 copy.82
  321.4 1.7 slice_reduce_fusion
  (63 shorter events, 4.1 us)
Async XLA Ops:
  7.2 1.4 copy-start.1
  7.2 218.2 %all-reduce.4.cloned.1.call-start = ((), (), s32[]{:S(2)}) async-start(), calls=%async_computation.2 | async-start | bytes 8912896
  8.6 3.1 copy-start.2
  11.7 4.8 %copy-start.12 = (bf16[1,1024]{1,0:T(2,128)(2,1)S(1)}, bf16[1,1024]{1,0:T(2,128)(2,1)}, u32[]{:S(2)}) copy-start(bf16[1,1024]{1,0:T(2,128)(2,1)} %param.19) | copy-start | bytes 6148
  16.5 2.3 copy-start
  26.3 0.7 copy-start.15
  26.4 1.9 copy-start.3
  26.4 2.0 copy-start.6
  26.4 2.2 copy-start.4
  26.4 2.2 copy-start.5
  26.4 206.3 %copy-start.13 = (f32[16]{0:T(128)S(1)}, f32[16]{0:T(128)}, u32[]{:S(2)}) copy-start(f32[16]{0:T(128)} %param.24) | copy-start | bytes 196
  26.4 206.3 %copy-start.14 = (f32[16]{0:T(128)S(1)}, f32[16]{0:T(128)}, u32[]{:S(2)}) copy-start(f32[16]{0:T(128)} %param.29) | copy-start | bytes 196
  26.4 209.6 %copy-start.8 = (f32[16,256]{1,0:T(8,128)S(1)}, f32[16,256]{1,0:T(8,128)}, u32[]{:S(2)}) copy-start(f32[16,256]{1,0:T(8,128)} %param.25) | copy-start | bytes 49156
  26.4 210.3 %copy-start.9 = (f32[16,256]{1,0:T(8,128)S(1)}, f32[16,256]{1,0:T(8,128)}, u32[]{:S(2)}) copy-start(f32[16,256]{1,0:T(8,128)} %param.26) | copy-start | bytes 49156
  26.4 211.0 %copy-start.10 = (f32[16,256]{1,0:T(8,128)S(1)}, f32[16,256]{1,0:T(8,128)}, u32[]{:S(2)}) copy-start(f32[16,256]{1,0:T(8,128)} %param.27) | copy-start | bytes 49156
  26.4 211.6 %copy-start.11 = (f32[256,16]{0,1:T(8,128)S(1)}, f32[256,16]{0,1:T(8,128)}, u32[]{:S(2)}) copy-start(f32[256,16]{0,1:T(8,128)} %param.28) | copy-start | bytes 49156
  227.8 8.0 %all-to-all-start = ((f32[4,1,128]{2,1,0:T(1,128)}), f32[4,1,128]{2,1,0:T(1,128)S(1)}, u32[]{:S(2)}, u32[]{:S(2)}) async-start(f32[4,1,128]{2,1,0:T(1,128)} %broadcast_in_dim.3), calls=%async_computation | async-start | bytes 4096 | tf_op jit(solution)/shard_map/all_to_all | solution.py:31
  231.8 85.9 %all-gather.2.cloned.1.call-start = ((), (), s32[]{:S(2)}) async-start(), calls=%async_computation.1 | async-start | bytes 2396160 | tf_op jit(solution)/shard_map/all_gather | solution.py:51
  238.8 0.6 copy-start.7
Sparse Core Ops, SparseCore 0:
  26.6 198.7 all-reduce.3
  239.5 78.1 all-gather.1
where the time goes:
time: 331 us; the launch traced here: 330 us
  waiting for transfers between devices  278 us (84%)
  local copies, waits for them, and re-layouts  25.9 us (8%)
  between operations  14.9 us (5%)
  other arithmetic  7.53 us (2%)
  starting transfers between devices  4.01 us (1%)
    unnamed x3, waiting for transfers between devices  197 us
    all_gather x1, waiting for transfers between devices, turned_gather(): result = lax.all_gather(both, axis, axis=0, tiled=True)  78.3 us
  transfers between devices with their start and end apart: 3, of which 3 were waited for; matrix products, arithmetic and copies ran while one was open for 1% of the time, Pallas kernels for 0%

commit v1 on v0

--- a/solution.py
+++ b/solution.py
@@ -48,7 +48,9 @@
     turned = [jnp.moveaxis(a, dim, 0) for a, dim in zip(arrays, dims)]
     widths = [t[0].size for t in turned]
     both = jnp.concatenate([t.reshape(-1, w) for t, w in zip(turned, widths)], axis=1)
-    result = lax.all_gather(both, axis, axis=0, tiled=True)
+    result = jnp.concatenate(
+        lax.all_to_all(jnp.stack([both] * lax.axis_size(axis)), axis, 0, 0), axis=0
+    )
     blocks = jnp.split(result, [sum(widths[:k]) for k in range(1, len(widths))], axis=1)
     return tuple(
         (

time: 331 us -> 319 us (0.964)
  waiting for transfers between devices: 278 us -> 199 us
  blocking collectives: 0 us -> 69.4 us
    all_gather x1 -> x0, waiting for transfers between devices: 78.3 us -> none  [turned_gather(): result = lax.all_gather(both, axis, axis=0, tiled=True)]
    all_to_all x0 -> x1, blocking collectives: none -> 69.4 us  [turned_gather(): lax.all_to_all(jnp.stack([both] * lax.axis_size(axis)), axis, 0, 0)]
    unnamed x3 -> x2, waiting for transfers between devices: 197 us -> 197 us
  transfers between devices with their start and end apart: 3 -> 2, of which waited for: 3 -> 2; matrix products, arithmetic and copies ran while one was open for 1% -> 1% of each run, Pallas kernels for 0% -> 0%
where the time goes in v1:
time: 319 us; the launch traced here: 318 us
  waiting for transfers between devices  199 us (62%)
  blocking collectives  69.4 us (22%)
  local copies, waits for them, and re-layouts  23 us (7%)
  between operations  14.9 us (5%)
  other arithmetic  7.53 us (2%)
  starting transfers between devices  4.01 us (1%)
    unnamed x2, waiting for transfers between devices  197 us
    all_to_all x1, blocking collectives, turned_gather(): lax.all_to_all(jnp.stack([both] * lax.axis_size(axis)), axis, 0, 0)  69.4 us
  transfers between devices with their start and end apart: 2, of which 2 were waited for; matrix products, arithmetic and copies ran while one was open for 1% of the time, Pallas kernels for 0%

profile of v1, /device:TPU:1, one launch (start us, length us, event | category | flops | bytes accessed | tf_op | source)
XLA Modules:
  0.0 318.1 jit_solution(17220949708572399076)
XLA Ops:
  7.2 1.3 convert_element_type.42
  8.6 1.0 convert_element_type.43
  9.7 2.1 convert_element_type.44
  11.8 1.0 copy.78
  12.8 2.6 copy.79
  15.4 1.1 copy.80
  16.6 1.1 constant_dynamic-update-slice_fusion.3
  17.8 1.1 constant_dynamic-update-slice_fusion.2
  18.9 2.4 pad_convert_fusion
  21.3 5.0 %reshape.138 = f32[8704,128]{1,0:T(8,128)} reshape(f32[64,17408]{1,0:T(8,128)} %pad_convert_fusion) | data formatting | bytes 8912896 | tf_op jit(solution)/shard_map/reshape | solution.py:20
  28.6 196.8 %all-reduce.4.cloned.1.call-done = f32[8704,128]{1,0:T(8,128)} async-done(((f32[8704,128]{1,0:T(8,128)}), f32[8704,128]{1,0:T(8,128)}) %all-reduce.4.cloned.1.call-update) | async-done | bytes 4456464
  225.4 1.0 multiply_reduce_fusion.1
  227.3 0.6 broadcast_in_dim.3
  227.8 4.0 %all-to-all-start = ((f32[4,1,128]{2,1,0:T(1,128)}), f32[4,1,128]{2,1,0:T(1,128)S(1)}, u32[]{:S(2)}, u32[]{:S(2)}) async-start(f32[4,1,128]{2,1,0:T(1,128)} %broadcast_in_dim.3), calls=%async_computation | async-start | bytes 4096 | tf_op jit(solution)/shard_map/all_to_all | solution.py:31
  231.8 0.9 dynamic-slice_bitcast_fusion
  233.4 2.4 all-to-all-done
  236.0 0.7 constant_dynamic-update-slice_fusion.9
  236.7 0.7 constant_dynamic-update-slice_fusion.8
  237.4 0.7 constant_dynamic-update-slice_fusion.7
  238.1 0.7 constant_dynamic-update-slice_fusion.6
  239.0 69.4 %all_to_all.11 = bf16[64,16,1025]{2,1,0:T(8,128)(2,1)S(1)} all-to-all(bf16[64,16,1025]{2,1,0:T(8,128)(2,1)S(1)} %stack.2), channel_id=1, replica_groups=mesh['replica'=64,'model'=4] {'replica'}, dimensions={0} | all-to-all | bytes 4198400 | tf_op jit(solution)/shard_map/all_to_all | solution.py:52
  308.4 1.2 slice_bitcast_fusion
  309.5 0.7 slice_reduce_fusion
  310.3 1.0 copy.84
  (60 shorter events, 3.6 us)
Async XLA Ops:
  7.2 1.4 copy-start.1
  7.2 218.2 %all-reduce.4.cloned.1.call-start = ((), (), s32[]{:S(2)}) async-start(), calls=%async_computation.2 | async-start | bytes 8912896
  8.6 3.1 copy-start.2
  11.7 4.8 %copy-start.11 = (bf16[1,1024]{1,0:T(2,128)(2,1)S(1)}, bf16[1,1024]{1,0:T(2,128)(2,1)}, u32[]{:S(2)}) copy-start(bf16[1,1024]{1,0:T(2,128)(2,1)} %param.19) | copy-start | bytes 6148
  16.5 2.3 copy-start
  26.3 0.7 copy-start.14
  26.4 1.9 copy-start.3
  26.4 2.0 copy-start.6
  26.4 2.2 copy-start.4
  26.4 2.2 copy-start.5
  26.4 206.3 %copy-start.12 = (f32[16]{0:T(128)S(1)}, f32[16]{0:T(128)}, u32[]{:S(2)}) copy-start(f32[16]{0:T(128)} %param.24) | copy-start | bytes 196
  26.4 206.3 %copy-start.13 = (f32[16]{0:T(128)S(1)}, f32[16]{0:T(128)}, u32[]{:S(2)}) copy-start(f32[16]{0:T(128)} %param.29) | copy-start | bytes 196
  26.4 209.6 %copy-start.7 = (f32[16,256]{1,0:T(8,128)S(1)}, f32[16,256]{1,0:T(8,128)}, u32[]{:S(2)}) copy-start(f32[16,256]{1,0:T(8,128)} %param.25) | copy-start | bytes 49156
  26.4 210.3 %copy-start.8 = (f32[16,256]{1,0:T(8,128)S(1)}, f32[16,256]{1,0:T(8,128)}, u32[]{:S(2)}) copy-start(f32[16,256]{1,0:T(8,128)} %param.26) | copy-start | bytes 49156
  26.4 211.0 %copy-start.9 = (f32[16,256]{1,0:T(8,128)S(1)}, f32[16,256]{1,0:T(8,128)}, u32[]{:S(2)}) copy-start(f32[16,256]{1,0:T(8,128)} %param.27) | copy-start | bytes 49156
  26.4 211.6 %copy-start.10 = (f32[256,16]{0,1:T(8,128)S(1)}, f32[256,16]{0,1:T(8,128)}, u32[]{:S(2)}) copy-start(f32[256,16]{0,1:T(8,128)} %param.28) | copy-start | bytes 49156
  227.8 8.0 %all-to-all-start = ((f32[4,1,128]{2,1,0:T(1,128)}), f32[4,1,128]{2,1,0:T(1,128)S(1)}, u32[]{:S(2)}, u32[]{:S(2)}) async-start(f32[4,1,128]{2,1,0:T(1,128)} %broadcast_in_dim.3), calls=%async_computation | async-start | bytes 4096 | tf_op jit(solution)/shard_map/all_to_all | solution.py:31
Sparse Core Ops, SparseCore 0:
  26.6 198.7 all-reduce.3
